TPU v7x, 32 devices: a whole 2x2x4 slice. The times are simulated.
32 devices in a mesh: grp: 1, win: 32 (over z, y, x, core).
Axes of the slice: x: 2, y: 2, z: 4, core: 2. Of those that a mesh axis runs over, the one named last changes fastest.
Arguments:
- tokens: bfloat16 [2, 8, 64, 96, 384], P('grp', None, None, 'win'), may hold values from -6 to 6
- w_upper: bfloat16 [384, 640], replicated, may hold values from -0.3125 to 0.3125
- w_surface: bfloat16 [384, 256], replicated, may hold values from -0.3125 to 0.3125
- bias: float32 [69], replicated, may hold values from -1 to 1
Outputs:
- fields: bfloat16 [2, 17664, 384], P('grp', 'win')
All inputs are finite; a program needn't handle non-finite values.
Results may differ from a plain program's by a relative error of at most 0.0048.
Values may be sent and summed in bfloat16 or wider, within the bound.
A program may use at most 128 MiB of HBM per device.

v0:
```python
import jax
import jax.numpy as jnp
from jax import lax
from jax.sharding import PartitionSpec as P

VARS_UP = 5
LEVELS = 13
VARS_SF = 4
PATCH = 4


def intersection_add(values, axis):
    first = lax.index_in_dim(values, 0, axis + 1, keepdims=False)
    second = lax.index_in_dim(values, 1, axis + 1, keepdims=False)
    pad_first = [(0, 0)] * first.ndim
    pad_second = [(0, 0)] * first.ndim
    pad_first[axis] = (0, 1)
    pad_second[axis] = (1, 0)
    return jnp.pad(first, pad_first) + jnp.pad(second, pad_second)


def latitude_add(values):
    first = values[..., 0, :, :]
    second = values[..., 1, :, :]
    pad_first = [(0, 0)] * (first.ndim - 1) + [(0, 1)]
    pad_second = [(0, 0)] * (first.ndim - 1) + [(1, 0)]
    summed = jnp.pad(first, pad_first) + jnp.pad(second, pad_second)
    return jnp.swapaxes(summed, -1, -2)


def project(tokens, w_upper, w_surface):
    members, tok_levels, lat_rows, lon_cols, width = tokens.shape
    upper_levels = tok_levels - 1
    rim_width = PATCH // 2
    frame_width = (lon_cols + 1) * PATCH
    upper_tok = jnp.transpose(tokens[:, :upper_levels], (0, 1, 3, 4, 2))
    kernel_up = w_upper.reshape(width, VARS_UP, 2, 2, PATCH, 2, PATCH)
    upper = jnp.einsum(
        "dvlpqrs,mzjdi->vlpqrsmzji", kernel_up, upper_tok, preferred_element_type=jnp.float32
    )
    upper = jnp.transpose(upper, (6, 8, 4, 5, 0, 7, 1, 2, 3, 9))
    upper = intersection_add(upper, 1)
    upper = latitude_add(upper)
    upper = upper.reshape(members, frame_width, VARS_UP, 2 * upper_levels, (lat_rows + 1) * PATCH)
    upper = upper[:, :, :, :LEVELS, rim_width : rim_width + lat_rows * PATCH]
    upper = upper.reshape(members, frame_width, VARS_UP * LEVELS, lat_rows * PATCH)
    surface_tok = jnp.transpose(tokens[:, upper_levels], (0, 2, 3, 1))
    kernel_sf = w_surface.reshape(width, VARS_SF, 2, PATCH, 2, PATCH)
    surface = jnp.einsum(
        "dvpqrs,mjdi->vpqrsmji", kernel_sf, surface_tok, preferred_element_type=jnp.float32
    )
    surface = jnp.transpose(surface, (5, 6, 3, 4, 0, 1, 2, 7))
    surface = intersection_add(surface, 1)
    surface = latitude_add(surface)
    surface = surface.reshape(members, frame_width, VARS_SF, (lat_rows + 1) * PATCH)
    surface = surface[:, :, :, rim_width : rim_width + lat_rows * PATCH]
    joined = jnp.concatenate([upper, surface], axis=2).astype(jnp.bfloat16)
    return joined.reshape(members, frame_width, -1)


def deliver(frames, bias, lat_rows):
    rim_width = PATCH // 2
    members, frame_width, all_rows = frames.shape
    columns = frame_width - 2 * rim_width
    windows = lax.axis_size("win")
    received = lax.all_to_all(frames, "win", split_axis=2, concat_axis=1, tiled=True)
    own_rows = received.shape[2]
    received = received.reshape(members, windows, frame_width, own_rows)
    inner = received[:, :, rim_width : frame_width - rim_width, :].astype(jnp.float32)
    from_left = jnp.roll(received[:, :, frame_width - rim_width :, :], 1, axis=1).astype(
        jnp.float32
    )
    from_right = jnp.roll(received[:, :, :rim_width, :], -1, axis=1).astype(jnp.float32)
    summed = inner + jnp.pad(from_left, ((0, 0), (0, 0), (0, columns - rim_width), (0, 0)))
    summed = summed + jnp.pad(from_right, ((0, 0), (0, 0), (columns - rim_width, 0), (0, 0)))
    first_row = lax.axis_index("win") * own_rows
    row_ids = first_row + jnp.arange(own_rows, dtype=jnp.int32)
    channel = row_ids // (lat_rows * PATCH)
    selector = (channel[:, None] == jnp.arange(bias.shape[0], dtype=jnp.int32)[None, :]).astype(
        jnp.float32
    )
    bias_rows = jnp.dot(selector, bias, precision=lax.Precision.HIGHEST)
    image = (summed + bias_rows[None, None, None, :]).astype(jnp.bfloat16)
    image = image.reshape(members, windows * columns, own_rows)
    return jnp.transpose(image, (0, 2, 1))


def body(tokens, w_upper, w_surface, bias):
    lat_rows = tokens.shape[2]
    frames = project(tokens, w_upper, w_surface)
    return deliver(frames, bias, lat_rows)


def solution(mesh):
    placed = (P("grp", None, None, "win", None), P(), P(), P())
    return jax.shard_map(
        body, mesh=mesh, in_specs=placed, out_specs=P("grp", "win", None), check_vma=False
    )
```

profile of v0, /device:TPU:0, one launch (start us, length us, event | category | flops | bytes accessed | tf_op | source)
XLA Modules:
  0.0 201.6 jit_solution(15619941665332143231)
XLA Ops:
  0.0 0.0 copy-start
  0.0 1.3 copy.25
  1.3 0.1 reshape.46
  1.4 7.7 %convolution_bitcast_fusion = f32[2,3,2,4,5,7,2,2,4,64]{9,4,1,5,0,3,2,8,7,6:T(8,128)S(1)} fusion(bf16[2,8,64,3,384]{4,2,3,1,0:T(8,128)(2,1)} %param.4, bf16[384,5,2,2,4,2,4,1,1,1]{0,6,5,4,3,2,1,9,8,7:T(4,128)(2,1)S(1)} %bitcast.81), kind=kOutput, calls=%fused_computation.4 | convolution fusion | flops 1321205760 | bytes 9437184 | tf_op jit(solution)/shard_map/dvlpqrs,mzjdi->vlpqrsmzji/dot_general | solution.py:38
  9.1 8.7 %slice_bitcast_fusion.1 = (f32[2,3,4,5,7,2,2,4,64]{8,3,1,4,0,2,7,6,5:T(8,128)}, f32[2,3,4,5,7,2,2,4,64]{8,3,1,4,0,2,7,6,5:T(8,128)}) fusion(f32[2,3,2,4,5,7,2,2,4,64]{9,4,1,5,0,3,2,8,7,6:T(8,128)S(1)} %convolution_bitcast_fusion), kind=kLoop, calls=%fused_computation.3 | loop fusion | bytes 13762560 | tf_op jit(solution)/shard_map/squeeze | solution.py:13
  17.8 12.0 %fusion.1 = (f32[2,4,4,5,7,2,4,64]{7,3,1,4,0,2,6,5:T(8,128)S(1)}, f32[2,4,4,5,7,2,4,64]{7,3,1,4,0,2,6,5:T(8,128)}) fusion(f32[2,3,4,5,7,2,2,4,64]{8,3,1,4,0,2,7,6,5:T(8,128)} %get-tuple-element.7, f32[2,3,4,5,7,2,2,4,64]{8,3,1,4,0,2,7,6,5:T(8,128)} %get-tuple-element.8), kind=kLoop, calls=%fused_computation.6 | loop fusion | flops 1146880 | bytes 11468800 | tf_op jit(solution)/shard_map/squeeze | solution.py:23
  29.9 6.9 %fusion.3 = bf16[2,4,4,5,7,2,65,4]{6,3,1,4,0,2,7,5:T(8,128)(2,1)} fusion(f32[2,4,4,5,7,2,4,64]{7,3,1,4,0,2,6,5:T(8,128)} %get-tuple-element.6, f32[2,4,4,5,7,2,4,64]{7,3,1,4,0,2,6,5:T(8,128)S(1)} %get-tuple-element.5), kind=kLoop, calls=%fused_computation.10 | loop fusion | flops 1164800 | bytes 5752320 | tf_op jit(solution)/shard_map/transpose | solution.py:28
  36.7 31.0 %copy.29 = bf16[2,4,4,5,7,2,65,4]{7,6,2,1,5,4,3,0:T(8,128)(2,1)} copy(bf16[2,4,4,5,7,2,65,4]{6,3,1,4,0,2,7,5:T(8,128)(2,1)} %fusion.3) | data formatting | bytes 2329600 | tf_op jit(solution)/shard_map/transpose | solution.py:28
  67.7 39.4 %reshape.47 = bf16[2,16,5,14,260]{4,1,3,2,0:T(8,128)(2,1)S(1)} reshape(bf16[2,4,4,5,7,2,65,4]{7,6,2,1,5,4,3,0:T(8,128)(2,1)} %copy.29) | data formatting | bytes 2329600 | tf_op jit(solution)/shard_map/reshape | solution.py:44
  107.0 0.5 slice.84
  107.5 0.0 copy-done.1
  107.5 0.2 copy.30
  107.7 0.1 reshape.54
  107.8 1.4 convolution_bitcast_fusion.1
  109.2 0.1 slice_bitcast_fusion.3
  109.3 0.2 fusion.16
  109.5 0.9 fusion.20
  110.4 2.0 %copy.34 = bf16[2,4,4,4,65,4]{5,4,2,1,3,0:T(8,128)(2,1)S(1)} copy(bf16[2,4,4,4,65,4]{4,2,1,0,5,3:T(4,128)(2,1)} %fusion.20) | data formatting | bytes 133120 | tf_op jit(solution)/shard_map/transpose | solution.py:28
  112.4 1.3 reshape.50
  113.7 0.1 slice.89
  113.8 0.1 pad_maximum_fusion
  113.9 13.7 %copy.46 = bf16[2,16,69,256]{1,0,3,2:T(2,128)(2,1)} copy(bf16[2,16,69,256]{3,1,2,0:T(8,128)(2,1)S(1)} %pad_maximum_fusion) | data formatting | bytes 2260992 | tf_op jit(solution)/shard_map/convert_element_type | solution.py:57
  127.6 11.7 %reshape.60 = bf16[32,2,8832]{2,1,0:T(2,128)(2,1)} reshape(bf16[17664,2,16]{2,1,0:T(2,128)(2,1)} %bitcast.74) | data formatting | bytes 2260992
  139.4 7.3 %all-to-all-start = ((bf16[32,2,8832]{2,1,0:T(2,128)(2,1)}), bf16[32,2,8832]{2,1,0:T(2,128)(2,1)S(1)}, u32[]{:S(2)}, u32[]{:S(2)}) async-start(bf16[32,2,8832]{2,1,0:T(2,128)(2,1)} %reshape.60), calls=%async_computation | async-start | bytes 2260992 | tf_op jit(solution)/shard_map/all_to_all | solution.py:66
  146.7 0.0 copy-done
  146.7 0.3 convolution_reduce_fusion
  147.1 27.6 %all-to-all-done = bf16[32,2,8832]{2,1,0:T(2,128)(2,1)S(1)} async-done(((bf16[32,2,8832]{2,1,0:T(2,128)(2,1)}), bf16[32,2,8832]{2,1,0:T(2,128)(2,1)S(1)}, u32[]{:S(2)}, u32[]{:S(2)}) %all-to-all-start) | async-done | bytes 1130528 | tf_op jit(solution)/shard_map/all_to_all | solution.py:66
  174.7 8.2 %reshape.61 = bf16[17664,2,16]{2,1,0:T(2,128)(2,1)} reshape(bf16[32,2,8832]{2,1,0:T(2,128)(2,1)S(1)} %all-to-all-done) | data formatting | bytes 2260992
  182.9 14.4 %copy.47 = bf16[2,16,32,552]{3,2,1,0:T(8,128)(2,1)S(1)} copy(bf16[2,16,32,552]{1,0,3,2:T(2,128)(2,1)} %bitcast.75) | data formatting | bytes 2260992 | tf_op jit(solution)/shard_map/all_to_all | solution.py:66
  197.4 0.3 add_convert_fusion.1
  197.7 1.0 copy.38
  198.7 2.9 %copy.39 = bf16[2,552,384]{2,1,0:T(8,128)(2,1)} copy(bf16[2,552,384]{1,0,2:T(2,128)(2,1)S(1)} %bitcast.80) | data formatting | bytes 1695744 | tf_op jit(solution)/shard_map/transpose | solution.py:85
  (4 shorter events, 0.1 us)
Async XLA Ops:
  0.0 146.7 %copy-start = (f32[69]{0:T(128)S(1)}, f32[69]{0:T(128)}, u32[]{:S(2)}) copy-start(f32[69]{0:T(128)} %param.7) | copy-start | bytes 832
  67.7 39.8 %copy-start.1 = (bf16[384,256]{1,0:T(8,128)(2,1)S(1)}, bf16[384,256]{1,0:T(8,128)(2,1)}, u32[]{:S(2)}) copy-start(bf16[384,256]{1,0:T(8,128)(2,1)} %param.6) | copy-start | bytes 589828
  139.4 35.3 %all-to-all-start = ((bf16[32,2,8832]{2,1,0:T(2,128)(2,1)}), bf16[32,2,8832]{2,1,0:T(2,128)(2,1)S(1)}, u32[]{:S(2)}, u32[]{:S(2)}) async-start(bf16[32,2,8832]{2,1,0:T(2,128)(2,1)} %reshape.60), calls=%async_computation | async-start | bytes 2260992 | tf_op jit(solution)/shard_map/all_to_all | solution.py:66
where the time goes:
time: 204 us; the launch traced here: 202 us
  local copies, waits for them, and re-layouts  137 us (67%)
  waiting for transfers between devices  27.6 us (14%)
  other arithmetic  20.3 us (10%)
  matrix products  9.46 us (5%)
  starting transfers between devices  7.33 us (4%)
    reshape x1, local copies, waits for them, and re-layouts, project(): upper.reshape(members, frame_width, VARS_UP, 2 * upper_levels, (lat_rows...  39.4 us
    transpose x2, local copies, waits for them, and re-layouts, latitude_add(): return jnp.swapaxes(summed, -1, -2)  33 us
    all_to_all x1, waiting for transfers between devices, deliver(): lax.all_to_all(frames, 'win', split_axis=2, concat_axis=1, tiled=True)  27.6 us
    unnamed x8, local copies, waits for them, and re-layouts  21.4 us
    all_to_all x1, local copies, waits for them, and re-layouts, deliver(): lax.all_to_all(frames, 'win', split_axis=2, concat_axis=1, tiled=True)  14.4 us
    convert_element_type x1, local copies, waits for them, and re-layouts, project(): joined = jnp.concatenate([upper, surface], axis=2).astype(jnp.bfloat16)  13.7 us
    squeeze x2, other arithmetic, latitude_add(): first = values[..., 0, :, :]  12.2 us
    squeeze x2, local copies, waits for them, and re-layouts, intersection_add(): first = lax.index_in_dim(values, 0, axis + 1, keepdims=False)  8.84 us
  transfers between devices with their start and end apart: 1, of which 1 were waited for; matrix products, arithmetic and copies ran while one was open for 0% of the time, Pallas kernels for 0%

commit v1 on v0

v1 whole, which is shorter than its diff:
```python
import functools

import jax
import jax.numpy as jnp
from jax import lax
from jax.experimental import pallas as pl
from jax.experimental.pallas import tpu as pltpu
from jax.sharding import PartitionSpec as P

VARS_UP = 5
LEVELS = 13
VARS_SF = 4
PATCH = 4
GROUP = 8
CHANNELS = VARS_UP * LEVELS + VARS_SF


def spans_of(owners, own_rows):
    return [
        (o * own_rows // PATCH, -(-(o + 1) * own_rows // PATCH)) for o in range(owners)
    ]


def selector(second, column):
    row = lax.broadcasted_iota(jnp.int32, (128, 128), 0)
    n = lax.broadcasted_iota(jnp.int32, (128, 128), 1)
    step = (n // 16) % 4 - column
    source = (n // 64) * 64 + (((n // 4) % 4 + 2 + 4 * second) % 8) * 8 + n % 4 + 4 * step
    hit = (row == source) & (step >= 0) & (step <= 1)
    return jnp.where(hit, 1.0, 0.0).astype(jnp.bfloat16)


def send_kernel(spans, pad_rows, tok_ref, wu_ref, ws_ref, wire_ref, wb_ref, y_ref, frame_ref):
    members, tok_levels, lon_cols, lat_rows, width = tok_ref.shape
    upper_levels = tok_levels - 1
    up_tiles = wu_ref.shape[1] // 128
    sf_tiles = ws_ref.shape[1] // 128
    sel = jnp.concatenate(
        [selector(y, j) for j in range(lon_cols) for y in range(2)], axis=1
    )
    for t in range(up_tiles + sf_tiles):
        if t < up_tiles:
            w = wu_ref[:, t * 128 : (t + 1) * 128]
        else:
            w = ws_ref[:, (t - up_tiles) * 128 : (t - up_tiles + 1) * 128]
        spread = jnp.dot(w, sel, preferred_element_type=jnp.float32).astype(jnp.bfloat16)
        for j in range(lon_cols):
            wb_ref[t, j * width : (j + 1) * width, :] = spread[:, j * 256 : (j + 1) * 256]
    lane = lax.broadcasted_iota(jnp.int32, (lat_rows, 128), 1)
    line = lax.broadcasted_iota(jnp.int32, (lat_rows, 128), 0)
    lower = (lane // 4) % 4 < 2
    low_lanes = lane < 64
    edge = jnp.where(lower, 0, lat_rows - 1)
    keep = line != edge

    def image(y):
        first, second = y[:, :128], y[:, 128:]
        moved = jnp.where(
            lower, pltpu.roll(second, 1, 0), pltpu.roll(second, lat_rows - 1, 0)
        )
        return first + jnp.where(keep, moved, 0.0)

    def put(channel, block):
        base = channel * lat_rows
        for o, (lo, hi) in enumerate(spans):
            a, b = max(lo, base), min(hi, base + lat_rows)
            if a < b:
                frame_ref[o, a - lo : b - lo, :] = block[a - base : b - base]

    def merge(even_channel, odd_channel, one, two):
        put(even_channel, jnp.where(low_lanes, one, pltpu.roll(two, 64, 1)))
        if odd_channel is not None:
            put(odd_channel, jnp.where(low_lanes, pltpu.roll(one, 64, 1), two))

    for t in range(up_tiles + sf_tiles):
        if t < up_tiles:
            levels = list(range(upper_levels))
        else:
            levels = [upper_levels]
        for m in range(members):
            z0, z1 = levels[0], levels[-1] + 1
            rows = (z1 - z0) * lat_rows
            total = None
            for j in range(lon_cols):
                part = jnp.dot(
                    tok_ref[m, z0:z1, j].reshape(rows, width),
                    wb_ref[t, j * width : (j + 1) * width, :],
                    preferred_element_type=jnp.float32,
                )
                total = part if total is None else total + part
            y_ref[m, :rows] = total
        for i, z in enumerate(levels):
            one, two = (
                image(y_ref[m, i * lat_rows : (i + 1) * lat_rows, :]) for m in range(members)
            )
            if t < up_tiles:
                even = t * LEVELS + 2 * z
                odd = even + 1 if 2 * z + 1 < LEVELS else None
            else:
                even = VARS_UP * LEVELS + 2 * (t - up_tiles)
                odd = even + 1
            merge(even, odd, one, two)
    wire_ref[...] = frame_ref[...].astype(jnp.bfloat16)


def compose(lat_rows, own_rows, got_ref, place_ref, bias_ref, out_ref, y_ref, image_ref):
    windows, pad_rows, _ = got_ref.shape
    members, _, lons = out_ref.shape
    groups = windows // GROUP
    tiles = lons // 128
    pitch = lons // groups
    for g in range(groups):
        stacked = jnp.concatenate([got_ref[g * GROUP + i] for i in range(GROUP)], axis=1)
        y_ref[g] = jnp.dot(stacked, place_ref[...], preferred_element_type=jnp.float32)
    lane = lax.broadcasted_iota(jnp.int32, (pad_rows, 128), 1)
    for m in range(members):
        for q in range(PATCH):
            sums = [None] * tiles
            at = (m * PATCH + q) * 128

            def add(tile, value):
                tile = tile % tiles
                sums[tile] = value if sums[tile] is None else sums[tile] + value

            for g in range(groups):
                start = g * pitch - PATCH // 2
                shift = start % 128
                value = y_ref[g, :, at : at + 128]
                if shift:
                    value = pltpu.roll(value, shift, 1)
                if shift + pitch + PATCH <= 128:
                    add(start // 128, value)
                else:
                    add(start // 128, jnp.where(lane >= shift, value, 0.0))
                    add(start // 128 + 1, jnp.where(lane < shift, value, 0.0))
            for tile in range(tiles):
                image_ref[m, tile, pl.ds(q, pad_rows, stride=PATCH), :] = sums[tile]
    first_row = lax.axis_index("win") * own_rows
    height = lat_rows * PATCH
    row = first_row + lax.broadcasted_iota(jnp.int32, (own_rows, 128), 0)
    first = first_row // height
    last = bias_ref.shape[0] - 1
    offsets = jnp.zeros((own_rows, 128), jnp.float32)
    for i in range((own_rows - 1) // height + 2):
        channel = jnp.minimum(first + i, last)
        begins = (first + i) * height
        offsets = jnp.where(row >= begins, bias_ref[channel], offsets)
    begin = 0 if own_rows % PATCH == 0 else first_row % PATCH
    for m in range(members):
        for tile in range(tiles):
            rows = image_ref[m, tile, pl.ds(begin, own_rows), :]
            out_ref[m, :, tile * 128 : (tile + 1) * 128] = (rows + offsets).astype(jnp.bfloat16)


def placing(members, pitch):
    size = GROUP * 128
    row = lax.broadcasted_iota(jnp.int32, (size, size), 0)
    col = lax.broadcasted_iota(jnp.int32, (size, size), 1)
    target = (row // 64) % 2 * 512 + (row // 4) % 4 * 128
    target = target + row // 128 * pitch + (row // 16) % 4 * 4 + row % 4
    return (target == col).astype(jnp.bfloat16)


def body(tokens, w_upper, w_surface, bias):
    members, tok_levels, lat_rows, lon_cols, width = tokens.shape
    windows = lax.axis_size("win")
    own_rows = CHANNELS * lat_rows * PATCH // windows
    lons = windows * lon_cols * PATCH
    spans = spans_of(windows, own_rows)
    pad_rows = -(-max(hi - lo for lo, hi in spans) // 16) * 16
    tiles = w_upper.shape[1] // 128 + w_surface.shape[1] // 128
    wire = pl.pallas_call(
        functools.partial(send_kernel, spans, pad_rows),
        out_shape=jax.ShapeDtypeStruct((windows, pad_rows, 128), jnp.bfloat16),
        in_specs=[pl.BlockSpec(memory_space=pltpu.VMEM)] * 3,
        out_specs=pl.BlockSpec(memory_space=pltpu.VMEM),
        scratch_shapes=[
            pltpu.VMEM((tiles, lon_cols * width, 256), jnp.bfloat16),
            pltpu.VMEM((members, (tok_levels - 1) * lat_rows, 256), jnp.float32),
            pltpu.VMEM((windows, pad_rows, 128), jnp.float32),
        ],
        compiler_params=pltpu.CompilerParams(vmem_limit_bytes=32 * 1024 * 1024),
    )(jnp.transpose(tokens, (0, 1, 3, 2, 4)), w_upper, w_surface)
    got = lax.all_to_all(wire, "win", split_axis=0, concat_axis=0, tiled=True)
    place = placing(members, lon_cols * PATCH)
    return pl.pallas_call(
        functools.partial(compose, lat_rows, own_rows),
        out_shape=jax.ShapeDtypeStruct((members, own_rows, lons), jnp.bfloat16),
        in_specs=[
            pl.BlockSpec(memory_space=pltpu.VMEM),
            pl.BlockSpec(memory_space=pltpu.VMEM),
            pl.BlockSpec(memory_space=pltpu.SMEM),
        ],
        out_specs=pl.BlockSpec(memory_space=pltpu.VMEM),
        scratch_shapes=[
            pltpu.VMEM((windows // GROUP, pad_rows, GROUP * 128), jnp.float32),
            pltpu.VMEM((members, lons // 128, pad_rows * PATCH, 128), jnp.float32),
        ],
        compiler_params=pltpu.CompilerParams(vmem_limit_bytes=32 * 1024 * 1024),
    )(got, place, bias)


def solution(mesh):
    placed = (P("grp", None, None, "win", None), P(), P(), P())
    return jax.shard_map(
        body, mesh=mesh, in_specs=placed, out_specs=P("grp", "win", None), check_vma=False
    )
```

time: 204 us -> 50 us (0.25); the launches traced: 202 us -> 49.7 us
  local copies, waits for them, and re-layouts: 137 us -> 3.62 us
  other arithmetic: 20.3 us -> 3.68 us
  Pallas kernels: 0 us -> 9.69 us
  matrix products: 9.46 us -> 0 us
  waiting for transfers between devices: 27.6 us -> 25.3 us
    reshape x4 -> x0, local copies, waits for them, and re-layouts: 40.8 us -> none  [the longest x1 39.4 us: project(): upper.reshape(members, frame_width, VARS_UP, 2 * upper_levels, (lat_rows...]
    transpose x3 -> x0, local copies, waits for them, and re-layouts: 35.9 us -> none  [the longest x2 33 us: latitude_add(): return jnp.swapaxes(summed, -1, -2)]
    unnamed x8, local copies, waits for them, and re-layouts: 21.4 us -> 3.62 us
    convert_element_type x2 -> x0, local copies, waits for them, and re-layouts: 14.7 us -> none  [the longest x1 13.7 us: project(): joined = jnp.concatenate([upper, surface], axis=2).astype(jnp.bfloat16)]
    all_to_all x1 -> x0, local copies, waits for them, and re-layouts: 14.4 us -> none  [deliver(): lax.all_to_all(frames, 'win', split_axis=2, concat_axis=1, tiled=True)]
    squeeze x2 -> x0, other arithmetic: 12.2 us -> none  [latitude_add(): first = values[..., 0, :, :]]
    pallas_call x0 -> x2, Pallas kernels: none -> 9.69 us  [the longest x1 6.47 us: body(): pl.pallas_call(functools.partial(send_kernel, spans, pad_rows), out_shape...]
    dot_general x3 -> x0, matrix products: 9.46 us -> none  [the longest x1 7.67 us: project(): jnp.einsum('dvlpqrs,mzjdi->vlpqrsmzji', kernel_up, upper_tok, preferred_e...]
  transfers between devices with their start and end apart: 1 -> 1, of which waited for: 1 -> 1; matrix products, arithmetic and copies ran while one was open for 0% -> 7% of each run, Pallas kernels for 0% -> 0%
where the time goes in v1:
time: 50 us; the launch traced here: 49.7 us
  waiting for transfers between devices  25.3 us (51%)
  Pallas kernels  9.69 us (19%)
  starting transfers between devices  7.32 us (15%)
  other arithmetic  3.68 us (7%)
  local copies, waits for them, and re-layouts  3.62 us (7%)
    all_to_all x1, waiting for transfers between devices, body(): got = lax.all_to_all(wire, 'win', split_axis=0, concat_axis=0, tiled=True)  25.3 us
    all_to_all x1, starting transfers between devices, body(): got = lax.all_to_all(wire, 'win', split_axis=0, concat_axis=0, tiled=True)  7.32 us
    pallas_call x1, Pallas kernels, body(): pl.pallas_call(functools.partial(send_kernel, spans, pad_rows), out_shape...  6.47 us
    convert_element_type x1, other arithmetic, placing(): return (target == col).astype(jnp.bfloat16)  3.63 us
    unnamed x8, local copies, waits for them, and re-layouts  3.62 us
    pallas_call x1, Pallas kernels, body(): pl.pallas_call(functools.partial(compose, lat_rows, own_rows), out_shape=...  3.22 us
  transfers between devices with their start and end apart: 1, of which 1 were waited for; matrix products, arithmetic and copies ran while one was open for 7% of the time, Pallas kernels for 0%

profile of v1, /device:TPU:0, one launch (start us, length us, event | category | flops | bytes accessed | tf_op | source)
XLA Modules:
  0.0 49.7 jit_solution(8259738638082034047)
XLA Ops:
  0.0 0.0 copy-start
  0.0 1.7 %copy-done = bf16[2,8,64,3,384]{4,2,3,1,0:T(8,128)(2,1)S(1)} copy-done((bf16[2,8,64,3,384]{4,2,3,1,0:T(8,128)(2,1)S(1)}, bf16[2,8,64,3,384]{4,2,3,1,0:T(8,128)(2,1)}, u32[]{:S(2)}) %copy-start) | copy-done | bytes 2359320
  1.7 0.0 copy-start.1
  1.7 1.0 %copy-done.1 = bf16[384,640]{1,0:T(8,128)(2,1)S(1)} copy-done((bf16[384,640]{1,0:T(8,128)(2,1)S(1)}, bf16[384,640]{1,0:T(8,128)(2,1)}, u32[]{:S(2)}) %copy-start.1) | copy-done | bytes 491544
  2.7 0.0 copy-start.2
  2.7 0.9 %copy-done.2 = bf16[384,256]{1,0:T(8,128)(2,1)S(1)} copy-done((bf16[384,256]{1,0:T(8,128)(2,1)S(1)}, bf16[384,256]{1,0:T(8,128)(2,1)}, u32[]{:S(2)}) %copy-start.2) | copy-done | bytes 196632
  3.6 6.5 %shard_map.46 = bf16[32,144,128]{2,1,0:T(8,128)(2,1)} custom-call(bf16[2,8,3,64,384]{4,3,2,1,0:T(8,128)(2,1)S(1)} %bitcast.1, bf16[384,640]{1,0:T(8,128)(2,1)S(1)} %copy-done.1, bf16[384,256]{1,0:T(8,128)(2,1)S(1)} %copy-done.2), custom_call_target="tpu_custom_call" | custom-call | tf_op jit(solution)/shard_map/pallas_call | solution.py:172
  10.1 0.0 copy-start.3
  10.1 7.3 %all-to-all-start = ((bf16[32,144,128]{2,1,0:T(8,128)(2,1)}), bf16[32,144,128]{2,1,0:T(8,128)(2,1)S(1)}, u32[]{:S(2)}, u32[]{:S(2)}) async-start(bf16[32,144,128]{2,1,0:T(8,128)(2,1)} %shard_map.46), calls=%async_computation | async-start | bytes 2359296 | tf_op jit(solution)/shard_map/all_to_all | solution.py:184
  17.5 3.6 %fusion.11.place_ref = bf16[1024,1024]{1,0:T(8,128)(2,1)S(1)} fusion(s32[1024]{0:T(1024)S(1)} %get-tuple-element.8, s32[1024]{0:T(1024)S(1)} %get-tuple-element.10, s32[1024]{0:T(1024)S(1)} %get-tuple-element.5, s32[1024]{0:T(1024)S(1)} %get-tuple-element.15, s32[1024]{0:T(1024)S(1)} %get-tuple-element.6, s32[1024]{0:T(1024)S(1)} %get-tuple-element.16, ...), kind=kLoop, calls=%fused_computation.26 | loop fusion | flops 50331648 | bytes 2143232 | tf_op jit(solution)/shard_map/convert_element_type | solution.py:161
  21.2 25.3 %all-to-all-done.got_ref = bf16[32,144,128]{2,1,0:T(8,128)(2,1)S(1)} async-done(((bf16[32,144,128]{2,1,0:T(8,128)(2,1)}), bf16[32,144,128]{2,1,0:T(8,128)(2,1)S(1)}, u32[]{:S(2)}, u32[]{:S(2)}) %all-to-all-start) | async-done | bytes 1179680 | tf_op jit(solution)/shard_map/all_to_all | solution.py:184
  46.4 0.0 copy-done.3
  46.4 3.2 %shard_map.47 = bf16[2,552,384]{2,1,0:T(8,128)(2,1)} custom-call(bf16[32,144,128]{2,1,0:T(8,128)(2,1)S(1)} %all-to-all-done.got_ref, bf16[1024,1024]{1,0:T(8,128)(2,1)S(1)} %fusion.11.place_ref, f32[69]{0:T(128)S(1)} %copy-done.3), custom_call_target="tpu_custom_call" | custom-call | tf_op jit(solution)/shard_map/pallas_call | solution.py:186
  (8 shorter events, 0.0 us)
Async XLA Ops:
  0.0 1.7 %copy-start = (bf16[2,8,64,3,384]{4,2,3,1,0:T(8,128)(2,1)S(1)}, bf16[2,8,64,3,384]{4,2,3,1,0:T(8,128)(2,1)}, u32[]{:S(2)}) copy-start(bf16[2,8,64,3,384]{4,2,3,1,0:T(8,128)(2,1)} %param.4) | copy-start | bytes 7077892
  1.7 1.0 %copy-start.1 = (bf16[384,640]{1,0:T(8,128)(2,1)S(1)}, bf16[384,640]{1,0:T(8,128)(2,1)}, u32[]{:S(2)}) copy-start(bf16[384,640]{1,0:T(8,128)(2,1)} %wu_ref.1) | copy-start | bytes 1474564
  2.7 0.9 %copy-start.2 = (bf16[384,256]{1,0:T(8,128)(2,1)S(1)}, bf16[384,256]{1,0:T(8,128)(2,1)}, u32[]{:S(2)}) copy-start(bf16[384,256]{1,0:T(8,128)(2,1)} %ws_ref.1) | copy-start | bytes 589828
  10.1 36.3 %copy-start.3 = (f32[69]{0:T(128)S(1)}, f32[69]{0:T(128)}, u32[]{:S(2)}) copy-start(f32[69]{0:T(128)} %bias_ref.1) | copy-start | bytes 832
  10.1 36.3 %all-to-all-start = ((bf16[32,144,128]{2,1,0:T(8,128)(2,1)}), bf16[32,144,128]{2,1,0:T(8,128)(2,1)S(1)}, u32[]{:S(2)}, u32[]{:S(2)}) async-start(bf16[32,144,128]{2,1,0:T(8,128)(2,1)} %shard_map.46), calls=%async_computation | async-start | bytes 2359296 | tf_op jit(solution)/shard_map/all_to_all | solution.py:184

commit v2 on v1

v2 whole, which is shorter than its diff:
```python
import functools

import jax
import jax.numpy as jnp
from jax import lax
from jax.experimental import pallas as pl
from jax.experimental.pallas import tpu as pltpu
from jax.sharding import PartitionSpec as P

VARS_UP = 5
LEVELS = 13
VARS_SF = 4
PATCH = 4
GROUP = 8
CHANNELS = VARS_UP * LEVELS + VARS_SF


def spans_of(owners, own_rows):
    return [
        (o * own_rows // PATCH, -(-(o + 1) * own_rows // PATCH)) for o in range(owners)
    ]


def selector(second, column):
    row = lax.broadcasted_iota(jnp.int32, (128, 128), 0)
    n = lax.broadcasted_iota(jnp.int32, (128, 128), 1)
    step = (n // 16) % 4 - column
    source = (n // 64) * 64 + (((n // 4) % 4 + 2 + 4 * second) % 8) * 8 + n % 4 + 4 * step
    hit = (row == source) & (step >= 0) & (step <= 1)
    return jnp.where(hit, 1.0, 0.0).astype(jnp.bfloat16)


def partner(me, r, windows):
    if windows & (windows - 1):
        return lax.rem(me + r, windows)
    return me ^ r


def kernel(
    own_rows, tok_hbm, wu_hbm, ws_hbm, bias_ref, out_ref,
    tok_ref, wu_ref, ws_ref, wb_ref, proj_ref, frame_ref, wire_ref, got_ref, place_ref,
    y_ref, image_ref, load_sem, send_sem, recv_sem,
):
    members, tok_levels, lon_cols, lat_rows, width = tok_ref.shape
    windows, pad_rows, _ = wire_ref.shape
    upper_levels = tok_levels - 1
    up_tiles = wu_ref.shape[1] // 128
    sf_tiles = ws_ref.shape[1] // 128
    me = lax.axis_index("win")

    loads = [
        pltpu.make_async_copy(wu_hbm, wu_ref, load_sem.at[0]),
        pltpu.make_async_copy(ws_hbm, ws_ref, load_sem.at[1]),
        pltpu.make_async_copy(tok_hbm, tok_ref, load_sem.at[2]),
    ]
    for load in loads:
        load.start()

    barrier = pltpu.get_barrier_semaphore()

    def greet(r, carry):
        pl.semaphore_signal(
            barrier, inc=1, device_id={"win": partner(me, r, windows)},
            device_id_type=pl.DeviceIdType.MESH,
        )
        return carry

    lax.fori_loop(1, windows, greet, 0)

    sel = jnp.concatenate(
        [selector(y, j) for j in range(lon_cols) for y in range(2)], axis=1
    )
    loads[0].wait()
    loads[1].wait()
    for t in range(up_tiles + sf_tiles):
        if t < up_tiles:
            w = wu_ref[:, t * 128 : (t + 1) * 128]
        else:
            w = ws_ref[:, (t - up_tiles) * 128 : (t - up_tiles + 1) * 128]
        spread = jnp.dot(w, sel, preferred_element_type=jnp.float32).astype(jnp.bfloat16)
        for j in range(lon_cols):
            wb_ref[t, j * width : (j + 1) * width, :] = spread[:, j * 256 : (j + 1) * 256]
    lane = lax.broadcasted_iota(jnp.int32, (lat_rows, 128), 1)
    line = lax.broadcasted_iota(jnp.int32, (lat_rows, 128), 0)
    lower = (lane // 4) % 4 < 2
    low_lanes = lane < 64
    keep = line != jnp.where(lower, 0, lat_rows - 1)

    def image(y):
        first, second = y[:, :128], y[:, 128:]
        moved = jnp.where(
            lower, pltpu.roll(second, 1, 0), pltpu.roll(second, lat_rows - 1, 0)
        )
        return first + jnp.where(keep, moved, 0.0)

    def put(channel, block):
        start = pl.multiple_of(channel * lat_rows, 8)
        frame_ref[pl.ds(start, lat_rows), :] = block

    def multiply(tile, z0, z1):
        rows = (z1 - z0) * lat_rows
        for m in range(members):
            total = None
            for j in range(lon_cols):
                part = jnp.dot(
                    tok_ref[m, z0:z1, j].reshape(rows, width),
                    wb_ref[tile, j * width : (j + 1) * width, :],
                    preferred_element_type=jnp.float32,
                )
                total = part if total is None else total + part
            proj_ref[m, :rows] = total

    def merge(even_channel, odd_channel, i):
        one, two = (
            image(proj_ref[m, i * lat_rows : (i + 1) * lat_rows, :]) for m in range(members)
        )
        put(even_channel, jnp.where(low_lanes, one, pltpu.roll(two, 64, 1)))
        if odd_channel is not None:
            put(odd_channel, jnp.where(low_lanes, pltpu.roll(one, 64, 1), two))

    def copy_to(r):
        other = partner(me, r, windows)
        return pltpu.make_async_remote_copy(
            src_ref=wire_ref.at[other],
            dst_ref=got_ref.at[me],
            send_sem=send_sem.at[other],
            recv_sem=recv_sem.at[me],
            device_id={"win": other},
            device_id_type=pl.DeviceIdType.MESH,
        )

    def block_of(other):
        start = other * own_rows // PATCH
        return frame_ref[pl.ds(start, pad_rows), :].astype(jnp.bfloat16)

    def pack(r, carry):
        other = partner(me, r, windows)
        wire_ref[other] = block_of(other)
        return carry

    def send(r, carry):
        copy_to(r).start()
        return carry

    tail = CHANNELS * lat_rows
    frame_ref[tail:, :] = jnp.zeros((frame_ref.shape[0] - tail, 128), jnp.float32)
    loads[2].wait()
    for t in range(sf_tiles):
        multiply(up_tiles + t, upper_levels, tok_levels)
        even = VARS_UP * LEVELS + 2 * t
        merge(even, even + 1, 0)
    early = up_tiles // 2 + 1
    turn = jnp.where(me < windows // 2, up_tiles - early, 0)
    half = windows // 2
    for slot in range(up_tiles):
        t = lax.rem(slot + turn, up_tiles)
        multiply(t, 0, upper_levels)
        for z in range(upper_levels):
            even = t * LEVELS + 2 * z
            merge(even, even + 1 if 2 * z + 1 < LEVELS else None, z)
        if slot == early - 1:
            lax.fori_loop(half, windows, pack, 0)
            pl.semaphore_wait(barrier, windows - 1)
            lax.fori_loop(half, windows, send, 0)
    lax.fori_loop(1, half, pack, 0)
    lax.fori_loop(1, half, send, 0)
    got_ref[me] = block_of(me)

    lons = out_ref.shape[2]
    groups = windows // GROUP
    pitch = lons // windows
    row = lax.broadcasted_iota(jnp.int32, (128, GROUP * 128), 0)
    col = lax.broadcasted_iota(jnp.int32, (128, GROUP * 128), 1)
    target = row // 64 * 512 + (row // 4) % 4 * 128 + (row // 16) % 4 * 4 + row % 4

    def fill(i, carry):
        hit = col == target + i * pitch
        place_ref[pl.ds(pl.multiple_of(i * 128, 128), 128), :] = jnp.where(
            hit, 1.0, 0.0
        ).astype(jnp.bfloat16)
        return carry

    lax.fori_loop(0, GROUP, fill, 0)

    def arrived(source):
        pltpu.make_async_remote_copy(
            src_ref=wire_ref.at[source],
            dst_ref=got_ref.at[source],
            send_sem=send_sem.at[source],
            recv_sem=recv_sem.at[source],
            device_id={"win": source},
            device_id_type=pl.DeviceIdType.MESH,
        ).wait_recv()

    def gather(k, carry):
        g = partner(me // GROUP, k, groups)

        def wait_one(i, inner):
            source = g * GROUP + i

            @pl.when(source != me)
            def _():
                arrived(source)

            return inner

        lax.fori_loop(0, GROUP, wait_one, 0)
        stacked = jnp.concatenate([got_ref[g * GROUP + i] for i in range(GROUP)], axis=1)
        y_ref[g] = jnp.dot(stacked, place_ref[...], preferred_element_type=jnp.float32)
        return carry

    lax.fori_loop(0, groups, gather, 0)
    compose(lat_rows, own_rows, me, bias_ref, out_ref, y_ref, image_ref)

    def sent(r, carry):
        copy_to(r).wait_send()
        return carry

    lax.fori_loop(1, windows, sent, 0)


def compose(lat_rows, own_rows, me, bias_ref, out_ref, y_ref, image_ref):
    groups, pad_rows, _ = y_ref.shape
    members, _, lons = out_ref.shape
    tiles = lons // 128
    pitch = lons // groups
    lane = lax.broadcasted_iota(jnp.int32, (pad_rows, 128), 1)
    for m in range(members):
        for q in range(PATCH):
            sums = [None] * tiles
            at = (m * PATCH + q) * 128

            def add(tile, value):
                tile = tile % tiles
                sums[tile] = value if sums[tile] is None else sums[tile] + value

            for g in range(groups):
                start = g * pitch - PATCH // 2
                shift = start % 128
                value = y_ref[g, :, at : at + 128]
                if shift:
                    value = pltpu.roll(value, shift, 1)
                if shift + pitch + PATCH <= 128:
                    add(start // 128, value)
                else:
                    add(start // 128, jnp.where(lane >= shift, value, 0.0))
                    add(start // 128 + 1, jnp.where(lane < shift, value, 0.0))
            for tile in range(tiles):
                image_ref[m, tile, pl.ds(q, pad_rows, stride=PATCH), :] = sums[tile]
    first_row = me * own_rows
    height = lat_rows * PATCH
    row = first_row + lax.broadcasted_iota(jnp.int32, (own_rows, 128), 0)
    first = first_row // height
    last = bias_ref.shape[0] - 1
    offsets = jnp.zeros((own_rows, 128), jnp.float32)
    for i in range((own_rows - 1) // height + 2):
        channel = jnp.minimum(first + i, last)
        begins = (first + i) * height
        offsets = jnp.where(row >= begins, bias_ref[channel], offsets)
    begin = 0 if own_rows % PATCH == 0 else first_row % PATCH
    for m in range(members):
        for tile in range(tiles):
            rows = image_ref[m, tile, pl.ds(begin, own_rows), :]
            out_ref[m, :, tile * 128 : (tile + 1) * 128] = (rows + offsets).astype(jnp.bfloat16)


def body(tokens, w_upper, w_surface, bias):
    members, tok_levels, lat_rows, lon_cols, width = tokens.shape
    windows = lax.axis_size("win")
    own_rows = CHANNELS * lat_rows * PATCH // windows
    lons = windows * lon_cols * PATCH
    spans = spans_of(windows, own_rows)
    pad_rows = -(-max(hi - lo for lo, hi in spans) // 16) * 16
    frame_rows = -(-(spans[-1][0] + pad_rows) // 8) * 8
    tiles = w_upper.shape[1] // 128 + w_surface.shape[1] // 128
    groups = windows // GROUP
    bf16, f32 = jnp.bfloat16, jnp.float32
    by_lon = jnp.transpose(tokens, (0, 1, 3, 2, 4))
    return pl.pallas_call(
        functools.partial(kernel, own_rows),
        out_shape=jax.ShapeDtypeStruct((members, own_rows, lons), bf16),
        in_specs=[pl.BlockSpec(memory_space=pltpu.HBM)] * 3
        + [pl.BlockSpec(memory_space=pltpu.SMEM)],
        out_specs=pl.BlockSpec(memory_space=pltpu.VMEM),
        scratch_shapes=[
            pltpu.VMEM(by_lon.shape, bf16),
            pltpu.VMEM(w_upper.shape, bf16),
            pltpu.VMEM(w_surface.shape, bf16),
            pltpu.VMEM((tiles, lon_cols * width, 256), bf16),
            pltpu.VMEM((members, (tok_levels - 1) * lat_rows, 256), f32),
            pltpu.VMEM((frame_rows, 128), f32),
            pltpu.VMEM((windows, pad_rows, 128), bf16),
            pltpu.VMEM((windows, pad_rows, 128), bf16),
            pltpu.VMEM((GROUP * 128, GROUP * 128), bf16),
            pltpu.VMEM((groups, pad_rows, GROUP * 128), f32),
            pltpu.VMEM((members, lons // 128, pad_rows * PATCH, 128), f32),
            pltpu.SemaphoreType.DMA((3,)),
            pltpu.SemaphoreType.DMA((windows,)),
            pltpu.SemaphoreType.DMA((windows,)),
        ],
        compiler_params=pltpu.CompilerParams(
            collective_id=0, has_side_effects=True, vmem_limit_bytes=65 * 1000 * 1000
        ),
    )(by_lon, w_upper, w_surface, bias)


def solution(mesh):
    placed = (P("grp", None, None, "win", None), P(), P(), P())
    return jax.shard_map(
        body, mesh=mesh, in_specs=placed, out_specs=P("grp", "win", None), check_vma=False
    )
```

time: 50 us -> 40.8 us (0.82)
  the two profiles are of different devices: /device:TPU:0 before, /device:TPU:9 now
where the time goes in v2:
time: 40.8 us; the launch traced here: 40.6 us
  Pallas kernels  38.5 us (94%)
  local copies, waits for them, and re-layouts  2.14 us (5%)
    pallas_call x1, Pallas kernels, body(): pl.pallas_call(functools.partial(kernel, own_rows), out_shape=jax.ShapeDt...  38.5 us
    unnamed x1, local copies, waits for them, and re-layouts  2.14 us

profile of v2, /device:TPU:9, one launch (start us, length us, event | category | flops | bytes accessed | tf_op | source)
XLA Modules:
  0.0 40.6 jit_solution(850815009268319098)
XLA Ops:
  0.0 38.5 %shard_map.46 = bf16[2,552,384]{2,1,0:T(8,128)(2,1)} custom-call(bf16[2,8,3,64,384]{4,3,2,1,0:T(8,128)(2,1)} %bitcast.1, bf16[384,640]{1,0:T(8,128)(2,1)} %wu_hbm.1, bf16[384,256]{1,0:T(8,128)(2,1)} %ws_hbm.1, f32[69]{0:T(128)} %bias_ref.1), custom_call_target="tpu_custom_call" | custom-call | tf_op jit(solution)/shard_map/pallas_call | solution.py:279
  38.5 2.1 %copy.6 = bf16[2,552,384]{2,1,0:T(8,128)(2,1)} copy(bf16[2,552,384]{2,1,0:T(8,128)(2,1)} %shard_map.46) | data formatting | bytes 1695744

commit v3 on v2

v3 whole, which is shorter than its diff:
```python
import functools

import jax
import jax.numpy as jnp
from jax import lax
from jax.experimental import pallas as pl
from jax.experimental.pallas import tpu as pltpu
from jax.sharding import PartitionSpec as P

VARS_UP = 5
LEVELS = 13
VARS_SF = 4
PATCH = 4
GROUP = 8
CHANNELS = VARS_UP * LEVELS + VARS_SF


def spans_of(owners, own_rows):
    return [
        (o * own_rows // PATCH, -(-(o + 1) * own_rows // PATCH)) for o in range(owners)
    ]


def selector(second, column):
    row = lax.broadcasted_iota(jnp.int32, (128, 128), 0)
    n = lax.broadcasted_iota(jnp.int32, (128, 128), 1)
    step = (n // 16) % 4 - column
    source = (n // 64) * 64 + (((n // 4) % 4 + 2 + 4 * second) % 8) * 8 + n % 4 + 4 * step
    hit = (row == source) & (step >= 0) & (step <= 1)
    return jnp.where(hit, 1.0, 0.0).astype(jnp.bfloat16)


def partner(me, r, windows):
    if windows & (windows - 1):
        return lax.rem(me + r, windows)
    return me ^ r


def kernel(
    plan, tok_hbm, wu_hbm, ws_hbm, bias_ref, out_ref,
    tok_ref, wu_ref, ws_ref, wb_ref, proj_ref, frame_ref, wire_ref, got_ref, place_ref, image_ref,
    load_sem, send_sem, recv_sem,
):
    members, tok_levels, lon_cols, lat_rows, width = tok_ref.shape
    windows, pad_rows, _ = wire_ref.shape
    upper_levels = tok_levels - 1
    up_tiles = wu_ref.shape[1] // 128
    sf_tiles = ws_ref.shape[1] // 128
    me = lax.axis_index("win")

    loads = [
        pltpu.make_async_copy(wu_hbm, wu_ref, load_sem.at[0]),
        pltpu.make_async_copy(ws_hbm, ws_ref, load_sem.at[1]),
        pltpu.make_async_copy(tok_hbm, tok_ref, load_sem.at[2]),
    ]
    for load in loads:
        load.start()

    barrier = pltpu.get_barrier_semaphore()

    def greet(r, carry):
        pl.semaphore_signal(
            barrier, inc=1, device_id={"win": partner(me, r, windows)},
            device_id_type=pl.DeviceIdType.MESH,
        )
        return carry

    lax.fori_loop(1, windows, greet, 0)

    own_rows, low_plan, high_plan = plan
    sel = jnp.concatenate(
        [selector(y, j) for j in range(lon_cols) for y in range(2)], axis=1
    )

    def spread(w):
        wide = jnp.dot(w, sel, preferred_element_type=jnp.float32).astype(jnp.bfloat16)
        for j in range(lon_cols):
            wb_ref[j * width : (j + 1) * width, :] = wide[:, j * 256 : (j + 1) * 256]

    lane = lax.broadcasted_iota(jnp.int32, (lat_rows, 128), 1)
    line = lax.broadcasted_iota(jnp.int32, (lat_rows, 128), 0)
    lower = (lane // 4) % 4 < 2
    low_lanes = lane < 64
    keep = line != jnp.where(lower, 0, lat_rows - 1)

    def image(y):
        first, second = y[:, :128], y[:, 128:]
        moved = jnp.where(
            lower, pltpu.roll(second, 1, 0), pltpu.roll(second, lat_rows - 1, 0)
        )
        return first + jnp.where(keep, moved, 0.0)

    def put(channel, block):
        start = pl.multiple_of(channel * lat_rows, 8)
        frame_ref[pl.ds(start, lat_rows), :] = block

    def multiply(z0, z1):
        rows = (z1 - z0) * lat_rows
        for m in range(members):
            total = None
            for j in range(lon_cols):
                part = jnp.dot(
                    tok_ref[m, z0:z1, j].reshape(rows, width),
                    wb_ref[j * width : (j + 1) * width, :],
                    preferred_element_type=jnp.float32,
                )
                total = part if total is None else total + part
            proj_ref[m, :rows] = total

    def merge(even_channel, odd_channel, i):
        one, two = (
            image(proj_ref[m, i * lat_rows : (i + 1) * lat_rows, :]) for m in range(members)
        )
        put(even_channel, jnp.where(low_lanes, one, pltpu.roll(two, 64, 1)))
        if odd_channel is not None:
            put(odd_channel, jnp.where(low_lanes, pltpu.roll(one, 64, 1), two))

    def copy_to(other):
        return pltpu.make_async_remote_copy(
            src_ref=wire_ref.at[other],
            dst_ref=got_ref.at[me],
            send_sem=send_sem.at[other],
            recv_sem=recv_sem.at[me],
            device_id={"win": other},
            device_id_type=pl.DeviceIdType.MESH,
        )

    def block_of(other):
        start = other * own_rows // PATCH
        return frame_ref[pl.ds(start, pad_rows), :].astype(jnp.bfloat16)

    low = me < windows // 2

    def deliver(slot):
        begin, count, more, extra = (
            jnp.where(low, a, b) for a, b in zip(low_plan[slot], high_plan[slot])
        )
        total = count + extra

        def owner(i):
            i = lax.rem(i + me, jnp.maximum(total, 1))
            return jnp.where(i < count, begin + i, more + i - count)

        def pack(i, carry):
            other = owner(i)
            wire_ref[other] = block_of(other)
            return carry

        def send(i, carry):
            other = owner(i)

            @pl.when(other != me)
            def _():
                copy_to(other).start()

            return carry

        lax.fori_loop(0, total, pack, 0)
        if slot == 0:
            pl.semaphore_wait(barrier, windows - 1)
        lax.fori_loop(0, total, send, 0)

    tail = CHANNELS * lat_rows
    frame_ref[tail:, :] = jnp.zeros((frame_ref.shape[0] - tail, 128), jnp.float32)
    loads[0].wait()
    for slot in range(up_tiles):
        t = jnp.where(low, up_tiles - 1 - slot, slot)
        spread(wu_ref[:, pl.ds(pl.multiple_of(t * 128, 128), 128)])
        if slot == 0:
            loads[1].wait()
            loads[2].wait()
        multiply(0, upper_levels)
        for z in range(upper_levels):
            even = t * LEVELS + 2 * z
            merge(even, even + 1 if 2 * z + 1 < LEVELS else None, z)
        if slot == 1:
            for u in range(sf_tiles):
                spread(ws_ref[:, u * 128 : (u + 1) * 128])
                multiply(upper_levels, tok_levels)
                even = VARS_UP * LEVELS + 2 * u
                merge(even, even + 1, 0)
        deliver(slot)
    got_ref[me] = block_of(me)

    tiles = image_ref.shape[1]
    lons = tiles * 128
    groups = windows // GROUP
    pitch = lons // windows
    row = lax.broadcasted_iota(jnp.int32, (128, GROUP * 128), 0)
    col = lax.broadcasted_iota(jnp.int32, (128, GROUP * 128), 1)
    target = row // 64 * 512 + (row // 4) % 4 * 128 + (row // 16) % 4 * 4 + row % 4

    def fill(i, carry):
        hit = col == target + i * pitch
        place_ref[pl.ds(pl.multiple_of(i * 128, 128), 128), :] = jnp.where(
            hit, 1.0, 0.0
        ).astype(jnp.bfloat16)
        return carry

    lax.fori_loop(0, GROUP, fill, 0)

    def arrived(source):
        pltpu.make_async_remote_copy(
            src_ref=wire_ref.at[source],
            dst_ref=got_ref.at[source],
            send_sem=send_sem.at[source],
            recv_sem=recv_sem.at[source],
            device_id={"win": source},
            device_id_type=pl.DeviceIdType.MESH,
        ).wait_recv()

    def gather(k, carry):
        g = partner(me // GROUP, k, groups)

        def wait_one(i, inner):
            source = g * GROUP + i

            @pl.when(source != me)
            def _():
                arrived(source)

            return inner

        lax.fori_loop(0, GROUP, wait_one, 0)
        stacked = jnp.concatenate([got_ref[g * GROUP + i] for i in range(GROUP)], axis=1)
        moved = jnp.dot(stacked, place_ref[...], preferred_element_type=jnp.float32)
        start = g * (GROUP * pitch) + (lons - PATCH // 2)
        shift = lax.rem(start, 128)
        tile = lax.rem(start // 128, tiles)
        after = lax.rem(tile + 1, tiles)
        first_part = lane_of_pad >= shift
        for m in range(members):
            for q in range(PATCH):
                at = (m * PATCH + q) * 128
                value = pltpu.roll(moved[:, at : at + 128], shift, 1)
                rows = pl.ds(q, pad_rows, stride=PATCH)
                image_ref[m, tile, rows, :] += jnp.where(first_part, value, 0.0)
                image_ref[m, after, rows, :] += jnp.where(first_part, 0.0, value)
        return carry

    lane_of_pad = lax.broadcasted_iota(jnp.int32, (pad_rows, 128), 1)
    image_ref[...] = jnp.zeros(image_ref.shape, jnp.float32)
    lax.fori_loop(0, groups, gather, 0)

    first_row = me * own_rows
    height = lat_rows * PATCH
    row = first_row + lax.broadcasted_iota(jnp.int32, (own_rows, 128), 0)
    first = first_row // height
    last = CHANNELS - 1
    offsets = jnp.zeros((own_rows, 128), jnp.float32)
    for i in range((own_rows - 1) // height + 2):
        channel = jnp.minimum(first + i, last)
        begins = (first + i) * height
        offsets = jnp.where(row >= begins, bias_ref[channel], offsets)
    begin = 0 if own_rows % PATCH == 0 else lax.rem(first_row, PATCH)
    for m in range(members):
        for tile in range(tiles):
            rows = image_ref[m, tile, pl.ds(begin, own_rows), :]
            out_ref[m, :, tile * 128 : (tile + 1) * 128] = (rows + offsets).astype(jnp.bfloat16)

    def sent(r, carry):
        copy_to(partner(me, r, windows)).wait_send()
        return carry

    lax.fori_loop(1, windows, sent, 0)


def write(held_ref, out_ref, sem):
    copies = [
        pltpu.make_async_copy(held_ref.at[m], out_ref.at[m], sem.at[m])
        for m in range(held_ref.shape[0])
    ]
    for copy in copies:
        copy.start()
    for copy in copies:
        copy.wait()


def plan_of(spans, lat_rows, tiles):
    owners, depth = len(spans), LEVELS * lat_rows
    surface = tiles * depth
    inner = [o for o in range(owners) if spans[o][1] <= surface]
    low, high = [], []
    done_low, done_high = inner[-1] + 1, 0
    for slot in range(tiles):
        floor = (tiles - 1 - slot) * depth
        begin = min(o for o in range(owners) if spans[o][0] >= floor)
        begin = min(begin, done_low)
        extra = owners - inner[-1] - 1 if slot == 1 else 0
        low.append((begin, done_low - begin, inner[-1] + 1, extra))
        done_low = begin
        ready = sum(1 for lo, hi in spans if hi <= (slot + 1) * depth)
        ready = owners if slot == tiles - 1 else ready
        high.append((done_high, ready - done_high, 0, 0))
        done_high = ready
    return low, high


def body(tokens, w_upper, w_surface, bias):
    members, tok_levels, lat_rows, lon_cols, width = tokens.shape
    windows = lax.axis_size("win")
    own_rows = CHANNELS * lat_rows * PATCH // windows
    lons = windows * lon_cols * PATCH
    spans = spans_of(windows, own_rows)
    pad_rows = -(-max(hi - lo for lo, hi in spans) // 16) * 16
    frame_rows = -(-(spans[-1][0] + pad_rows) // 8) * 8
    low_plan, high_plan = plan_of(spans, lat_rows, w_upper.shape[1] // 128)
    bf16, f32 = jnp.bfloat16, jnp.float32
    by_lon = jnp.transpose(tokens, (0, 1, 3, 2, 4))
    held = pl.pallas_call(
        functools.partial(kernel, (own_rows, low_plan, high_plan)),
        out_shape=jax.ShapeDtypeStruct((members, own_rows, lons), bf16),
        in_specs=[pl.BlockSpec(memory_space=pltpu.HBM)] * 3
        + [pl.BlockSpec(memory_space=pltpu.SMEM)],
        out_specs=pl.BlockSpec(memory_space=pltpu.VMEM),
        scratch_shapes=[
            pltpu.VMEM(by_lon.shape, bf16),
            pltpu.VMEM(w_upper.shape, bf16),
            pltpu.VMEM(w_surface.shape, bf16),
            pltpu.VMEM((lon_cols * width, 256), bf16),
            pltpu.VMEM((members, (tok_levels - 1) * lat_rows, 256), f32),
            pltpu.VMEM((frame_rows, 128), f32),
            pltpu.VMEM((windows, pad_rows, 128), bf16),
            pltpu.VMEM((windows, pad_rows, 128), bf16),
            pltpu.VMEM((GROUP * 128, GROUP * 128), bf16),
            pltpu.VMEM((members, lons // 128, pad_rows * PATCH, 128), f32),
            pltpu.SemaphoreType.DMA((3,)),
            pltpu.SemaphoreType.DMA((windows,)),
            pltpu.SemaphoreType.DMA((windows,)),
        ],
        compiler_params=pltpu.CompilerParams(
            collective_id=0, has_side_effects=True, vmem_limit_bytes=65 * 1000 * 1000
        ),
    )(by_lon, w_upper, w_surface, bias)
    return pl.pallas_call(
        write,
        out_shape=jax.ShapeDtypeStruct((members, own_rows, lons), bf16),
        in_specs=[pl.BlockSpec(memory_space=pltpu.VMEM)],
        out_specs=pl.BlockSpec(memory_space=pl.ANY),
        scratch_shapes=[pltpu.SemaphoreType.DMA((members,))],
    )(held)


def solution(mesh):
    placed = (P("grp", None, None, "win", None), P(), P(), P())
    return jax.shard_map(
        body, mesh=mesh, in_specs=placed, out_specs=P("grp", "win", None), check_vma=False
    )
```

time: 40.8 us -> 37.6 us (0.922)
  the two profiles are of different devices: /device:TPU:9 before, /device:TPU:15 now
where the time goes in v3:
time: 37.6 us; the launch traced here: 37.4 us
  Pallas kernels  37.4 us (99%)
    pallas_call x1, Pallas kernels, body(): pl.pallas_call(functools.partial(kernel, (own_rows, low_plan, high_plan))...  35.3 us
    pallas_call x1, Pallas kernels, body(): pl.pallas_call(write, out_shape=jax.ShapeDtypeStruct((members, own_rows,...  2.07 us

profile of v3, /device:TPU:15, one launch (start us, length us, event | category | flops | bytes accessed | tf_op | source)
XLA Modules:
  0.0 37.4 jit_solution(6157772317852259862)
XLA Ops:
  0.0 35.3 %shard_map.46.held_ref = bf16[2,552,384]{2,1,0:T(8,128)(2,1)} custom-call(bf16[2,8,3,64,384]{4,3,2,1,0:T(8,128)(2,1)} %bitcast.1, bf16[384,640]{1,0:T(8,128)(2,1)} %wu_hbm.1, bf16[384,256]{1,0:T(8,128)(2,1)} %ws_hbm.1, f32[69]{0:T(128)} %bias_ref.1), custom_call_target="tpu_custom_call" | custom-call | tf_op jit(solution)/shard_map/pallas_call | solution.py:310
  35.3 2.1 %shard_map.47 = bf16[2,552,384]{2,1,0:T(8,128)(2,1)} custom-call(bf16[2,552,384]{2,1,0:T(8,128)(2,1)} %shard_map.46.held_ref), custom_call_target="tpu_custom_call" | custom-call | tf_op jit(solution)/shard_map/pallas_call | solution.py:335

commit v4 on v3

--- a/solution.py
+++ b/solution.py
@@ -265,14 +265,27 @@
     lax.fori_loop(1, windows, sent, 0)
 
 
-def write(held_ref, out_ref, sem):
-    copies = [
-        pltpu.make_async_copy(held_ref.at[m], out_ref.at[m], sem.at[m])
-        for m in range(held_ref.shape[0])
+def write(held_hbm, out_hbm, part_ref, sem):
+    members, cuts, _, lanes = part_ref.shape
+    pieces = [(m, i) for m in range(members) for i in range(cuts)]
+
+    def view(ref, m, i):
+        return ref.at[m, :, i * lanes : (i + 1) * lanes]
+
+    reads = [
+        pltpu.make_async_copy(view(held_hbm, m, i), part_ref.at[m, i], sem.at[0, m, i])
+        for m, i in pieces
     ]
-    for copy in copies:
+    writes = [
+        pltpu.make_async_copy(part_ref.at[m, i], view(out_hbm, m, i), sem.at[1, m, i])
+        for m, i in pieces
+    ]
+    for read in reads:
+        read.start()
+    for read, copy in zip(reads, writes):
+        read.wait()
         copy.start()
-    for copy in copies:
+    for copy in writes:
         copy.wait()
 
 
@@ -335,9 +348,12 @@
     return pl.pallas_call(
         write,
         out_shape=jax.ShapeDtypeStruct((members, own_rows, lons), bf16),
-        in_specs=[pl.BlockSpec(memory_space=pltpu.VMEM)],
+        in_specs=[pl.BlockSpec(memory_space=pl.ANY)],
         out_specs=pl.BlockSpec(memory_space=pl.ANY),
-        scratch_shapes=[pltpu.SemaphoreType.DMA((members,))],
+        scratch_shapes=[
+            pltpu.VMEM((members, 3, own_rows, lons // 3), bf16),
+            pltpu.SemaphoreType.DMA((2, members, 3)),
+        ],
     )(held)
 
 

time: 37.6 us -> 37.5 us (level)
  no operation moved by 1% of the time
where the time goes in v4:
time: 37.5 us; the launch traced here: 37.3 us
  Pallas kernels  37.3 us (99%)
    pallas_call x1, Pallas kernels, body(): pl.pallas_call(functools.partial(kernel, (own_rows, low_plan, high_plan))...  35.3 us
    pallas_call x1, Pallas kernels, body(): pl.pallas_call(write, out_shape=jax.ShapeDtypeStruct((members, own_rows,...  2 us

profile of v4, /device:TPU:15, one launch (start us, length us, event | category | flops | bytes accessed | tf_op | source)
XLA Modules:
  0.0 37.3 jit_solution(17756726793564838321)
XLA Ops:
  0.0 35.3 %shard_map.46.held_hbm = bf16[2,552,384]{2,1,0:T(8,128)(2,1)} custom-call(bf16[2,8,3,64,384]{4,3,2,1,0:T(8,128)(2,1)} %bitcast.1, bf16[384,640]{1,0:T(8,128)(2,1)} %wu_hbm.1, bf16[384,256]{1,0:T(8,128)(2,1)} %ws_hbm.1, f32[69]{0:T(128)} %bias_ref.1), custom_call_target="tpu_custom_call" | custom-call | tf_op jit(solution)/shard_map/pallas_call | solution.py:323
  35.3 2.0 %shard_map.47 = bf16[2,552,384]{2,1,0:T(8,128)(2,1)} custom-call(bf16[2,552,384]{2,1,0:T(8,128)(2,1)} %shard_map.46.held_hbm), custom_call_target="tpu_custom_call" | custom-call | tf_op jit(solution)/shard_map/pallas_call | solution.py:348
